TPU v7x, 32 devices: a whole 2x2x4 slice. The times are simulated.
32 devices in a mesh: owner: 4 (over y, core), rows: 8 (over z, x).
Axes of the slice: x: 2, y: 2, z: 4, core: 2. Of those that a mesh axis runs over, the one named last changes fastest.
Arguments:
- train_gate: float32 [128, 2048, 768], P('owner', 'rows'), may hold values from -0.125 to 0.125
- train_up: float32 [128, 2048, 768], P('owner', 'rows'), may hold values from -0.125 to 0.125
- router_weight: float32 [2048, 128], P('rows', 'owner'), may hold values from -0.125 to 0.125
- router_gain: float32 [2048], P('rows'), may hold values from 0.25 to 1.75
Outputs:
- ready_gate: bfloat16 [128, 768, 2048], P(('owner', 'rows'))
- ready_up: bfloat16 [128, 768, 2048], P(('owner', 'rows'))
- serve_router: bfloat16 [2048, 128], replicated
All inputs are finite; a program needn't handle non-finite values.
Results may differ from a plain program's by a relative error of at most 0.001.
Values may be sent and summed in bfloat16 or wider, within the bound.
A program may use at most 192 MiB of HBM per device.

v0:
```python
import jax
import jax.numpy as jnp
from jax import lax
from jax.sharding import PartitionSpec as P


def on_device(train_gate, train_up, router_weight, router_gain):
    narrow_gate, narrow_up = (train_gate.astype(jnp.bfloat16), train_up.astype(jnp.bfloat16))
    ready_gate, ready_up = (
        lax.all_to_all(narrow_gate, "rows", split_axis=0, concat_axis=1, tiled=True),
        lax.all_to_all(narrow_up, "rows", split_axis=0, concat_axis=1, tiled=True),
    )
    ready_gate = jnp.transpose(ready_gate, (0, 2, 1))
    ready_up = jnp.transpose(ready_up, (0, 2, 1))
    part_router = (router_weight * router_gain[:, None]).astype(jnp.bfloat16)
    row_router = lax.all_gather(part_router, "rows", axis=0, tiled=True)
    serve_router = lax.all_gather(row_router, "owner", axis=1, tiled=True)
    return (ready_gate, ready_up, serve_router)


def solution(mesh):
    placed = (P("owner", "rows", None), P("owner", "rows", None), P("rows", "owner"), P("rows"))
    return jax.shard_map(
        on_device,
        mesh=mesh,
        in_specs=placed,
        out_specs=(P(("owner", "rows"), None, None), P(("owner", "rows"), None, None), P()),
        check_vma=False,
    )
```

profile of v0, /device:TPU:0, one launch (start us, length us, event | category | flops | bytes accessed | tf_op | source)
XLA Modules:
  0.0 672.7 jit_solution(13268045616997217038)
XLA Ops:
  0.6 13.2 %convert_element_type.9 = bf16[32,256,768]{2,1,0:T(8,128)(2,1)} convert(f32[32,256,768]{2,1,0:T(8,128)} %param.4) | non-fusion elementwise | flops 6291456 | bytes 37748736 | tf_op jit(solution)/shard_map/convert_element_type | solution.py:8
  13.8 7.3 %all-to-all-start = ((bf16[32,256,768]{2,1,0:T(8,128)(2,1)}), bf16[32,256,768]{2,1,0:T(8,128)(2,1)}, u32[]{:S(2)}, u32[]{:S(2)}) async-start(bf16[32,256,768]{2,1,0:T(8,128)(2,1)} %convert_element_type.9), calls=%async_computation | async-start | bytes 25165824 | tf_op jit(solution)/shard_map/all_to_all | solution.py:10
  21.1 13.4 %convert_element_type.10 = bf16[32,256,768]{2,1,0:T(8,128)(2,1)} convert(f32[32,256,768]{2,1,0:T(8,128)} %param.5) | non-fusion elementwise | flops 6291456 | bytes 37748736 | tf_op jit(solution)/shard_map/convert_element_type | solution.py:8
  34.5 0.0 copy-start
  34.5 0.0 copy-start.1
  34.5 259.7 %all-to-all-done = bf16[32,256,768]{2,1,0:T(8,128)(2,1)} async-done(((bf16[32,256,768]{2,1,0:T(8,128)(2,1)}), bf16[32,256,768]{2,1,0:T(8,128)(2,1)}, u32[]{:S(2)}, u32[]{:S(2)}) %all-to-all-start) | async-done | bytes 12582944 | tf_op jit(solution)/shard_map/all_to_all | solution.py:10
  294.2 5.3 all-to-all-start.1
  299.5 0.0 copy-done
  299.5 0.0 copy-done.1
  299.5 292.2 %all_gather.6 = bf16[2048,32]{0,1:T(8,128)(2,1)S(1)} all-gather(bf16[256,32]{0,1:T(8,128)(2,1)S(1)} %multiply_convert_fusion), channel_id=1, replica_groups=mesh['owner'=4,'rows'=8] {'rows'}, dimensions={0}, use_global_device_ids=true | all-gather | bytes 147456 | tf_op jit(solution)/shard_map/all_gather | solution.py:16
  591.8 7.2 %all_gather.7 = bf16[2048,128]{0,1:T(8,128)(2,1)S(1)} all-gather(bf16[2048,32]{0,1:T(8,128)(2,1)S(1)} %all_gather.6), channel_id=1, replica_groups=mesh['owner'=4,'rows'=8] {'owner'}, dimensions={1}, use_global_device_ids=true | all-gather | bytes 655360 | tf_op jit(solution)/shard_map/all_gather | solution.py:17
  598.9 1.0 copy.12
  599.9 16.9 %copy.10 = bf16[8,4,256,768]{2,0,3,1:T(8,128)(2,1)} copy(bf16[8,4,256,768]{3,2,1,0:T(8,128)(2,1)} %bitcast) | data formatting | bytes 25165824 | tf_op jit(solution)/shard_map/all_to_all | solution.py:10
  616.8 19.5 %all_to_all.29 = bf16[4,2048,768]{1,2,0:T(8,128)(2,1)} reshape(bf16[4,8,256,768]{2,1,3,0:T(8,128)(2,1)} %bitcast.14) | data formatting | bytes 25165824 | tf_op jit(solution)/shard_map/all_to_all | solution.py:10
  636.3 0.0 all-to-all-done.1
  636.3 16.9 %copy.11 = bf16[8,4,256,768]{2,0,3,1:T(8,128)(2,1)} copy(bf16[8,4,256,768]{3,2,1,0:T(8,128)(2,1)} %bitcast.3) | data formatting | bytes 25165824 | tf_op jit(solution)/shard_map/all_to_all | solution.py:11
  653.2 19.5 %all_to_all.33 = bf16[4,2048,768]{1,2,0:T(8,128)(2,1)} reshape(bf16[4,8,256,768]{2,1,3,0:T(8,128)(2,1)} %bitcast.15) | data formatting | bytes 25165824 | tf_op jit(solution)/shard_map/all_to_all | solution.py:11
  (1 shorter events, 0.0 us)
Async XLA Ops:
  13.8 280.3 %all-to-all-start = ((bf16[32,256,768]{2,1,0:T(8,128)(2,1)}), bf16[32,256,768]{2,1,0:T(8,128)(2,1)}, u32[]{:S(2)}, u32[]{:S(2)}) async-start(bf16[32,256,768]{2,1,0:T(8,128)(2,1)} %convert_element_type.9), calls=%async_computation | async-start | bytes 25165824 | tf_op jit(solution)/shard_map/all_to_all | solution.py:10
  34.5 265.0 %copy-start = (f32[256,32]{0,1:T(8,128)S(1)}, f32[256,32]{0,1:T(8,128)}, u32[]{:S(2)}) copy-start(f32[256,32]{0,1:T(8,128)} %param.6) | copy-start | bytes 98308
  34.5 265.0 %copy-start.1 = (f32[256]{0:T(256)S(1)}, f32[256]{0:T(256)}, u32[]{:S(2)}) copy-start(f32[256]{0:T(256)} %param.7) | copy-start | bytes 3076
  294.2 342.1 %all-to-all-start.1 = ((bf16[32,256,768]{2,1,0:T(8,128)(2,1)}), bf16[32,256,768]{2,1,0:T(8,128)(2,1)}, u32[]{:S(2)}, u32[]{:S(2)}) async-start(bf16[32,256,768]{2,1,0:T(8,128)(2,1)} %convert_element_type.10), calls=%async_computation.1 | async-start | bytes 25165824 | tf_op jit(solution)/shard_map/all_to_all | solution.py:11
where the time goes:
time: 675 us; the launch traced here: 673 us
  blocking collectives  299 us (44%)
  waiting for transfers between devices  260 us (39%)
  local copies, waits for them, and re-layouts  73.7 us (11%)
  other arithmetic  26.6 us (4%)
  starting transfers between devices  12.6 us (2%)
    all_gather x1, blocking collectives, on_device(): row_router = lax.all_gather(part_router, 'rows', axis=0, tiled=True)  292 us
    all_to_all x1, waiting for transfers between devices, on_device(): lax.all_to_all(narrow_gate, 'rows', split_axis=0, concat_axis=1, tiled=True)  260 us
    all_to_all x2, local copies, waits for them, and re-layouts, on_device(): lax.all_to_all(narrow_up, 'rows', split_axis=0, concat_axis=1, tiled=True)  36.4 us
    all_to_all x2, local copies, waits for them, and re-layouts, on_device(): lax.all_to_all(narrow_gate, 'rows', split_axis=0, concat_axis=1, tiled=True)  36.3 us
  transfers between devices with their start and end apart: 2, of which 1 were waited for; matrix products, arithmetic and copies ran while one was open for 5% of the time, Pallas kernels for 0%

commit v1 on v0

--- a/solution.py
+++ b/solution.py
@@ -13,7 +13,9 @@
     ready_gate = jnp.transpose(ready_gate, (0, 2, 1))
     ready_up = jnp.transpose(ready_up, (0, 2, 1))
     part_router = (router_weight * router_gain[:, None]).astype(jnp.bfloat16)
-    row_router = lax.all_gather(part_router, "rows", axis=0, tiled=True)
+    row_router = jnp.concatenate(
+        lax.all_to_all(jnp.stack([part_router] * lax.axis_size("rows")), "rows", 0, 0), axis=0
+    )
     serve_router = lax.all_gather(row_router, "owner", axis=1, tiled=True)
     return (ready_gate, ready_up, serve_router)
 

time: 675 us -> 616 us (0.913)
  blocking collectives: 299 us -> 7.2 us
  waiting for transfers between devices: 260 us -> 486 us
    all_gather x1 -> x0, blocking collectives: 292 us -> none  [on_device(): row_router = lax.all_gather(part_router, 'rows', axis=0, tiled=True)]
    all_to_all x1, waiting for transfers between devices: 0.01 us -> 227 us  [on_device(): lax.all_to_all(narrow_up, 'rows', split_axis=0, concat_axis=1, tiled=True)]
    all_to_all x0 -> x1, starting transfers between devices: none -> 7.28 us  [on_device(): lax.all_to_all(jnp.stack([part_router] * lax.axis_size('rows')), 'rows',...]
  transfers between devices with their start and end apart: 2 -> 3, of which waited for: 1 -> 2; matrix products, arithmetic and copies ran while one was open for 5% -> 7% of each run, Pallas kernels for 0% -> 0%
where the time goes in v1:
time: 616 us; the launch traced here: 614 us
  waiting for transfers between devices  486 us (79%)
  local copies, waits for them, and re-layouts  74.4 us (12%)
  other arithmetic  27.3 us (4%)
  starting transfers between devices  18.6 us (3%)
  blocking collectives  7.2 us (1%)
    all_to_all x1, waiting for transfers between devices, on_device(): lax.all_to_all(narrow_gate, 'rows', split_axis=0, concat_axis=1, tiled=True)  259 us
    all_to_all x1, waiting for transfers between devices, on_device(): lax.all_to_all(narrow_up, 'rows', split_axis=0, concat_axis=1, tiled=True)  227 us
    all_to_all x2, local copies, waits for them, and re-layouts, on_device(): lax.all_to_all(narrow_up, 'rows', split_axis=0, concat_axis=1, tiled=True)  36.4 us
    all_to_all x2, local copies, waits for them, and re-layouts, on_device(): lax.all_to_all(narrow_gate, 'rows', split_axis=0, concat_axis=1, tiled=True)  36.3 us
    convert_element_type x1, other arithmetic, on_device(): train_up.astype(jnp.bfloat16)  13.4 us
    convert_element_type x1, other arithmetic, on_device(): train_gate.astype(jnp.bfloat16)  13.2 us
  transfers between devices with their start and end apart: 3, of which 2 were waited for; matrix products, arithmetic and copies ran while one was open for 7% of the time, Pallas kernels for 0%

profile of v1, /device:TPU:0, one launch (start us, length us, event | category | flops | bytes accessed | tf_op | source)
XLA Modules:
  0.0 614.3 jit_solution(1102473876650567153)
XLA Ops:
  0.6 0.8 multiply_convert_fusion
  1.4 0.7 stack.2
  2.1 7.3 %all-to-all-start.2 = ((bf16[8,256,32]{1,2,0:T(8,128)(2,1)}), bf16[8,256,32]{1,2,0:T(8,128)(2,1)S(1)}, u32[]{:S(2)}, u32[]{:S(2)}) async-start(bf16[8,256,32]{1,2,0:T(8,128)(2,1)} %stack.2), calls=%async_computation.2 | async-start | bytes 262144 | tf_op jit(solution)/shard_map/all_to_all | solution.py:17
  9.3 13.2 %convert_element_type.9 = bf16[32,256,768]{2,1,0:T(8,128)(2,1)} convert(f32[32,256,768]{2,1,0:T(8,128)} %param.4) | non-fusion elementwise | flops 6291456 | bytes 37748736 | tf_op jit(solution)/shard_map/convert_element_type | solution.py:8
  22.5 0.0 all-to-all-done.2
  22.5 6.0 all-to-all-start
  28.5 13.4 %convert_element_type.10 = bf16[32,256,768]{2,1,0:T(8,128)(2,1)} convert(f32[32,256,768]{2,1,0:T(8,128)} %param.5) | non-fusion elementwise | flops 6291456 | bytes 37748736 | tf_op jit(solution)/shard_map/convert_element_type | solution.py:8
  41.9 259.1 %all-to-all-done = bf16[32,256,768]{2,1,0:T(8,128)(2,1)} async-done(((bf16[32,256,768]{2,1,0:T(8,128)(2,1)}), bf16[32,256,768]{2,1,0:T(8,128)(2,1)}, u32[]{:S(2)}, u32[]{:S(2)}) %all-to-all-start) | async-done | bytes 12582944 | tf_op jit(solution)/shard_map/all_to_all | solution.py:10
  301.0 5.3 all-to-all-start.1
  306.4 7.2 %all_gather.3 = bf16[2048,128]{0,1:T(8,128)(2,1)S(1)} all-gather(bf16[2048,32]{0,1:T(8,128)(2,1)S(1)} %bitcast.20), channel_id=1, replica_groups=mesh['owner'=4,'rows'=8] {'owner'}, dimensions={1}, use_global_device_ids=true | all-gather | bytes 655360 | tf_op jit(solution)/shard_map/all_gather | solution.py:19
  313.6 1.0 copy.16
  314.6 16.9 %copy.13 = bf16[8,4,256,768]{2,0,3,1:T(8,128)(2,1)} copy(bf16[8,4,256,768]{3,2,1,0:T(8,128)(2,1)} %bitcast) | data formatting | bytes 25165824 | tf_op jit(solution)/shard_map/all_to_all | solution.py:10
  331.5 19.5 %all_to_all.32 = bf16[4,2048,768]{1,2,0:T(8,128)(2,1)} reshape(bf16[4,8,256,768]{2,1,3,0:T(8,128)(2,1)} %bitcast.16) | data formatting | bytes 25165824 | tf_op jit(solution)/shard_map/all_to_all | solution.py:10
  350.9 227.0 %all-to-all-done.1 = bf16[32,256,768]{2,1,0:T(8,128)(2,1)} async-done(((bf16[32,256,768]{2,1,0:T(8,128)(2,1)}), bf16[32,256,768]{2,1,0:T(8,128)(2,1)}, u32[]{:S(2)}, u32[]{:S(2)}) %all-to-all-start.1) | async-done | bytes 12582944 | tf_op jit(solution)/shard_map/all_to_all | solution.py:11
  578.0 16.9 %copy.14 = bf16[8,4,256,768]{2,0,3,1:T(8,128)(2,1)} copy(bf16[8,4,256,768]{3,2,1,0:T(8,128)(2,1)} %bitcast.3) | data formatting | bytes 25165824 | tf_op jit(solution)/shard_map/all_to_all | solution.py:11
  594.8 19.5 %all_to_all.36 = bf16[4,2048,768]{1,2,0:T(8,128)(2,1)} reshape(bf16[4,8,256,768]{2,1,3,0:T(8,128)(2,1)} %bitcast.17) | data formatting | bytes 25165824 | tf_op jit(solution)/shard_map/all_to_all | solution.py:11
  (1 shorter events, 0.0 us)
Async XLA Ops:
  2.1 20.5 %all-to-all-start.2 = ((bf16[8,256,32]{1,2,0:T(8,128)(2,1)}), bf16[8,256,32]{1,2,0:T(8,128)(2,1)S(1)}, u32[]{:S(2)}, u32[]{:S(2)}) async-start(bf16[8,256,32]{1,2,0:T(8,128)(2,1)} %stack.2), calls=%async_computation.2 | async-start | bytes 262144 | tf_op jit(solution)/shard_map/all_to_all | solution.py:17
  22.5 278.5 %all-to-all-start = ((bf16[32,256,768]{2,1,0:T(8,128)(2,1)}), bf16[32,256,768]{2,1,0:T(8,128)(2,1)}, u32[]{:S(2)}, u32[]{:S(2)}) async-start(bf16[32,256,768]{2,1,0:T(8,128)(2,1)} %convert_element_type.9), calls=%async_computation | async-start | bytes 25165824 | tf_op jit(solution)/shard_map/all_to_all | solution.py:10
  301.0 276.9 %all-to-all-start.1 = ((bf16[32,256,768]{2,1,0:T(8,128)(2,1)}), bf16[32,256,768]{2,1,0:T(8,128)(2,1)}, u32[]{:S(2)}, u32[]{:S(2)}) async-start(bf16[32,256,768]{2,1,0:T(8,128)(2,1)} %convert_element_type.10), calls=%async_computation.1 | async-start | bytes 25165824 | tf_op jit(solution)/shard_map/all_to_all | solution.py:11

commit v2 on v0

--- a/solution.py
+++ b/solution.py
@@ -2,6 +2,17 @@
 import jax.numpy as jnp
 from jax import lax
 from jax.sharding import PartitionSpec as P
+
+
+def gather_around(x, axis, dim):
+    ways = lax.axis_size(axis)
+    pieces = [x]
+    for far in range(1, ways):
+        pieces.append(
+            lax.ppermute(pieces[far - 1], axis, [(d, (d - 1) % ways) for d in range(ways)])
+        )
+    line = jnp.concatenate(pieces, axis=dim)
+    return jnp.roll(line, lax.axis_index(axis) * x.shape[dim], axis=dim)
 
 
 def on_device(train_gate, train_up, router_weight, router_gain):
@@ -14,7 +25,7 @@
     ready_up = jnp.transpose(ready_up, (0, 2, 1))
     part_router = (router_weight * router_gain[:, None]).astype(jnp.bfloat16)
     row_router = lax.all_gather(part_router, "rows", axis=0, tiled=True)
-    serve_router = lax.all_gather(row_router, "owner", axis=1, tiled=True)
+    serve_router = gather_around(row_router, "owner", 1)
     return (ready_gate, ready_up, serve_router)
 
 

time: 675 us -> 680 us (level)
  blocking collectives: 299 us -> 292 us
  waiting for transfers between devices: 260 us -> 267 us
    ppermute x0 -> x3, waiting for transfers between devices: none -> 7.53 us  [gather_around(): lax.ppermute(pieces[far - 1], axis, [(d, (d - 1) % ways) for d in range(w...]
    all_gather x1 -> x0, blocking collectives: 7.19 us -> none  [on_device(): serve_router = lax.all_gather(row_router, 'owner', axis=1, tiled=True)]
  transfers between devices with their start and end apart: 2 -> 5, of which waited for: 1 -> 4; matrix products, arithmetic and copies ran while one was open for 5% -> 5% of each run, Pallas kernels for 0% -> 0%
where the time goes in v2:
time: 680 us; the launch traced here: 677 us
  blocking collectives  292 us (43%)
  waiting for transfers between devices  267 us (39%)
  local copies, waits for them, and re-layouts  73.9 us (11%)
  other arithmetic  26.6 us (4%)
  starting transfers between devices  16.4 us (2%)
    all_gather x1, blocking collectives, on_device(): row_router = lax.all_gather(part_router, 'rows', axis=0, tiled=True)  292 us
    all_to_all x1, waiting for transfers between devices, on_device(): lax.all_to_all(narrow_gate, 'rows', split_axis=0, concat_axis=1, tiled=True)  260 us
    all_to_all x2, local copies, waits for them, and re-layouts, on_device(): lax.all_to_all(narrow_up, 'rows', split_axis=0, concat_axis=1, tiled=True)  36.4 us
    all_to_all x2, local copies, waits for them, and re-layouts, on_device(): lax.all_to_all(narrow_gate, 'rows', split_axis=0, concat_axis=1, tiled=True)  36.3 us
  transfers between devices with their start and end apart: 5, of which 4 were waited for; matrix products, arithmetic and copies ran while one was open for 5% of the time, Pallas kernels for 0%

profile of v2, /device:TPU:0, one launch (start us, length us, event | category | flops | bytes accessed | tf_op | source)
XLA Modules:
  0.0 676.9 jit_solution(4411433780305559663)
XLA Ops:
  0.6 13.2 %convert_element_type.9 = bf16[32,256,768]{2,1,0:T(8,128)(2,1)} convert(f32[32,256,768]{2,1,0:T(8,128)} %param.4) | non-fusion elementwise | flops 6291456 | bytes 37748736 | tf_op jit(solution)/shard_map/convert_element_type | solution.py:19
  13.8 7.3 %all-to-all-start = ((bf16[32,256,768]{2,1,0:T(8,128)(2,1)}), bf16[32,256,768]{2,1,0:T(8,128)(2,1)}, u32[]{:S(2)}, u32[]{:S(2)}) async-start(bf16[32,256,768]{2,1,0:T(8,128)(2,1)} %convert_element_type.9), calls=%async_computation | async-start | bytes 25165824 | tf_op jit(solution)/shard_map/all_to_all | solution.py:21
  21.1 13.4 %convert_element_type.10 = bf16[32,256,768]{2,1,0:T(8,128)(2,1)} convert(f32[32,256,768]{2,1,0:T(8,128)} %param.5) | non-fusion elementwise | flops 6291456 | bytes 37748736 | tf_op jit(solution)/shard_map/convert_element_type | solution.py:19
  34.5 0.0 copy-start
  34.5 0.0 copy-start.1
  34.5 259.6 %all-to-all-done = bf16[32,256,768]{2,1,0:T(8,128)(2,1)} async-done(((bf16[32,256,768]{2,1,0:T(8,128)(2,1)}), bf16[32,256,768]{2,1,0:T(8,128)(2,1)}, u32[]{:S(2)}, u32[]{:S(2)}) %all-to-all-start) | async-done | bytes 12582944 | tf_op jit(solution)/shard_map/all_to_all | solution.py:21
  294.2 5.3 all-to-all-start.1
  299.5 0.0 copy-done
  299.5 0.0 copy-done.1
  299.5 292.2 %all_gather.3 = bf16[2048,32]{0,1:T(8,128)(2,1)S(1)} all-gather(bf16[256,32]{0,1:T(8,128)(2,1)S(1)} %multiply_convert_fusion), channel_id=1, replica_groups=mesh['owner'=4,'rows'=8] {'rows'}, dimensions={0}, use_global_device_ids=true | all-gather | bytes 147456 | tf_op jit(solution)/shard_map/all_gather | solution.py:27
  591.7 0.0 collective-permute-start
  591.8 2.5 collective-permute-done
  594.3 1.9 collective-permute-start.1
  596.2 2.5 collective-permute-done.1
  598.7 1.9 collective-permute-start.2
  600.6 2.5 collective-permute-done.2
  603.2 1.0 copy.12
  604.2 16.9 %copy.10 = bf16[8,4,256,768]{2,0,3,1:T(8,128)(2,1)} copy(bf16[8,4,256,768]{3,2,1,0:T(8,128)(2,1)} %bitcast) | data formatting | bytes 25165824 | tf_op jit(solution)/shard_map/all_to_all | solution.py:21
  621.1 19.5 %all_to_all.29 = bf16[4,2048,768]{1,2,0:T(8,128)(2,1)} reshape(bf16[4,8,256,768]{2,1,3,0:T(8,128)(2,1)} %bitcast.14) | data formatting | bytes 25165824 | tf_op jit(solution)/shard_map/all_to_all | solution.py:21
  640.5 0.0 all-to-all-done.1
  640.6 16.9 %copy.11 = bf16[8,4,256,768]{2,0,3,1:T(8,128)(2,1)} copy(bf16[8,4,256,768]{3,2,1,0:T(8,128)(2,1)} %bitcast.3) | data formatting | bytes 25165824 | tf_op jit(solution)/shard_map/all_to_all | solution.py:22
  657.5 19.5 %all_to_all.33 = bf16[4,2048,768]{1,2,0:T(8,128)(2,1)} reshape(bf16[4,8,256,768]{2,1,3,0:T(8,128)(2,1)} %bitcast.15) | data formatting | bytes 25165824 | tf_op jit(solution)/shard_map/all_to_all | solution.py:22
  (10 shorter events, 0.1 us)
Async XLA Ops:
  13.8 280.3 %all-to-all-start = ((bf16[32,256,768]{2,1,0:T(8,128)(2,1)}), bf16[32,256,768]{2,1,0:T(8,128)(2,1)}, u32[]{:S(2)}, u32[]{:S(2)}) async-start(bf16[32,256,768]{2,1,0:T(8,128)(2,1)} %convert_element_type.9), calls=%async_computation | async-start | bytes 25165824 | tf_op jit(solution)/shard_map/all_to_all | solution.py:21
  34.5 265.0 %copy-start = (f32[256,32]{0,1:T(8,128)S(1)}, f32[256,32]{0,1:T(8,128)}, u32[]{:S(2)}) copy-start(f32[256,32]{0,1:T(8,128)} %param.6) | copy-start | bytes 98308
  34.5 265.0 %copy-start.1 = (f32[256]{0:T(256)S(1)}, f32[256]{0:T(256)}, u32[]{:S(2)}) copy-start(f32[256]{0:T(256)} %param.7) | copy-start | bytes 3076
  294.2 346.4 %all-to-all-start.1 = ((bf16[32,256,768]{2,1,0:T(8,128)(2,1)}), bf16[32,256,768]{2,1,0:T(8,128)(2,1)}, u32[]{:S(2)}, u32[]{:S(2)}) async-start(bf16[32,256,768]{2,1,0:T(8,128)(2,1)} %convert_element_type.10), calls=%async_computation.1 | async-start | bytes 25165824 | tf_op jit(solution)/shard_map/all_to_all | solution.py:22
  591.7 2.5 collective-permute-start
  594.3 4.4 collective-permute-start.1
  598.7 4.4 collective-permute-start.2
